TPU v7x, 32 devices: a whole 2x2x4 slice. The times are simulated.
32 devices in a mesh: dp: 8 (over z, x), tp: 4 (over y, core).
Axes of the slice: x: 2, y: 2, z: 4, core: 2. Of those that a mesh axis runs over, the one named last changes fastest.
Arguments:
- gradients: bfloat16 [8, 4, 5120, 1280], P('dp', None, 'tp'), may hold values from -6 to 6
- right_factor: float32 [4, 1280, 32], replicated, may hold values from -6 to 6
- weights_before: float32 [4, 5120, 1280], P(None, 'tp', 'dp'), may hold values from -0.15625 to 0.15625
- momentum: float32 [4, 5120, 1280], P(None, 'tp', 'dp'), may hold values from -0.3125 to 0.3125
Outputs:
- new_weights: float32 [4, 5120, 1280], P(None, 'tp', 'dp')
- new_basis: float32 [4, 1280, 32], replicated
- new_momentum: float32 [4, 5120, 1280], P(None, 'tp', 'dp')
All inputs are finite; a program needn't handle non-finite values.
Results may differ from a plain program's by a relative error of at most 0.003.
Values sent between devices are 32-bit elements; how exact they have to be, the bound alone decides.
A program may use at most 64 MiB of HBM per device.

v0:
```python
import jax
import jax.numpy as jnp
from jax import lax
from jax.sharding import PartitionSpec as P

RANK = 32


def on_device(gradients, right_factor, weights_before, momentum):
    own_grads = gradients[0]
    part_left = jnp.einsum(
        "liw,lwr->lir",
        own_grads,
        right_factor.astype(jnp.bfloat16),
        preferred_element_type=jnp.float32,
    )
    left = lax.psum(part_left, "dp")
    part_gram = jnp.einsum("lir,lis->lrs", left, left, precision=lax.Precision.HIGHEST)
    small_left = left.astype(jnp.bfloat16)
    gram = lax.psum(part_gram, "tp")
    part_right = jnp.einsum(
        "liw,lir->lwr", own_grads, small_left, preferred_element_type=jnp.float32
    )
    right = lax.psum(part_right, ("dp", "tp"))
    gram = gram + 0.001 * jnp.mean(jnp.diagonal(gram, axis1=1, axis2=2), axis=1)[
        :, None, None
    ] * jnp.eye(RANK, dtype=jnp.float32)
    place = lax.axis_index("dp") * weights_before.shape[2]
    own_right = lax.dynamic_slice_in_dim(right, place, weights_before.shape[2], axis=1)
    root = jnp.linalg.cholesky(gram)
    half = lax.linalg.triangular_solve(
        root, jnp.swapaxes(own_right, 1, 2), left_side=True, lower=True
    )
    mixed = lax.linalg.triangular_solve(root, half, left_side=True, lower=True, transpose_a=True)
    change = jnp.einsum(
        "lir,lrw->liw", left, mixed, precision=lax.Precision.HIGHEST
    ) / lax.axis_size("dp")
    new_momentum = 0.8 * momentum + change
    new_weights = weights_before - 0.05 * new_momentum
    new_basis = right * lax.rsqrt(jnp.mean(right * right, axis=(1, 2), keepdims=True) + 1e-12)
    return (new_weights, new_basis, new_momentum)


def solution(mesh):
    return jax.shard_map(
        on_device,
        mesh=mesh,
        in_specs=(P("dp", None, "tp", None), P(), P(None, "tp", "dp"), P(None, "tp", "dp")),
        out_specs=(P(None, "tp", "dp"), P(), P(None, "tp", "dp")),
        check_vma=False,
    )
```

profile of v0, /device:TPU:0, one launch (start us, length us, event | category | flops | bytes accessed | tf_op | source)
XLA Modules:
  0.0 276.0 jit_solution(18249295536158250338)
XLA Ops:
  7.2 0.0 all-reduce.3.cloned.1.call-start
  7.2 9.6 %fusion.2 = f32[4,1280,32]{1,2,0:T(8,128)} fusion(bf16[1,4,1280,1280]{3,2,1,0:T(8,128)(2,1)} %param.4, f32[4,1280,32]{1,2,0:T(8,128)} %param.5), kind=kOutput, calls=%fused_computation.3 | convolution fusion | flops 419594240 | bytes 14417920 | tf_op jit(solution)/shard_map/liw,lwr->lir/dot_general | solution.py:11
  16.8 0.0 all-reduce.3.cloned.1.call-update
  16.8 0.0 all-reduce.5.cloned.1.call-start
  16.9 0.1 copy.13
  17.0 76.5 %all-reduce.3.cloned.1.call-done = f32[4,1280,32]{1,2,0:T(8,128)} async-done(((f32[4,1280,32]{1,2,0:T(8,128)}), f32[4,1280,32]{1,2,0:T(8,128)}) %all-reduce.3.cloned.1.call-update) | async-done | bytes 655376 | tf_op jit(solution)/shard_map/psum | solution.py:17
  93.4 2.0 fusion.18
  95.5 10.7 %psum.22 = f32[4,32,32]{1,2,0:T(8,128)S(1)} all-reduce(f32[4,32,32]{1,2,0:T(8,128)S(1)} %fusion.18), channel_id=1, replica_groups=mesh['dp'=8,'tp'=4] {'tp'}, use_global_device_ids=true, to_apply=%region_1.0 | all-reduce | flops 4096 | bytes 32768 | tf_op jit(solution)/shard_map/psum | solution.py:20
  106.1 0.5 copy.12
  106.7 0.7 gather_fusion
  107.4 0.1 multiply_add_fusion
  107.5 0.1 copy.14
  107.6 0.1 fusion.15
  107.7 11.7 %custom-call.9 = f32[4,32,32]{2,1,0:T(8,128)S(1)} custom-call(f32[4,32,32]{2,1,0:T(8,128)S(1)} %fusion.15), custom_call_target="Cholesky" | custom-call | tf_op jit(solution)/shard_map/jit(cholesky)/cholesky | solution.py:30
  119.4 8.1 %fusion.5 = f32[4,1280,32]{1,2,0:T(8,128)} fusion(bf16[1,4,1280,1280]{3,2,1,0:T(8,128)(2,1)} %param.4, f32[4,1280,32]{1,2,0:T(8,128)} %all-reduce.3.cloned.1.call-done), kind=kOutput, calls=%fused_computation.8 | convolution fusion | flops 419594240 | bytes 14417920 | tf_op jit(solution)/shard_map/liw,lir->lwr/dot_general | solution.py:21
  127.5 0.1 compare_reduce_fusion
  127.7 0.1 select_bitcast_fusion
  127.7 9.8 %custom-call.10 = f32[4,1,32,32]{2,3,1,0:T(8,128)S(1)} custom-call(f32[4,1,32,32]{3,2,1,0:T(8,128)S(1)} %select_bitcast_fusion), custom_call_target="InvertDiagBlocksLowerTriangular" | custom-call | tf_op jit(solution)/shard_map/triangular_solve | solution.py:34
  137.6 119.6 %all-reduce.5.cloned.1.call-done = f32[4,1280,32]{1,2,0:T(8,128)} async-done(((f32[4,1280,32]{1,2,0:T(8,128)}), f32[4,1280,32]{1,2,0:T(8,128)}) %all-reduce.5.cloned.1.call-update) | async-done | bytes 655376 | tf_op jit(solution)/shard_map/psum | solution.py:24
  257.2 1.2 multiply_reduce_fusion
  258.4 1.3 fusion.10
  259.7 0.3 fusion.12
  260.0 2.0 broadcast_multiply_fusion
  262.0 7.2 %multiply_subtract_fusion = (f32[4,1280,160]{1,2,0:T(8,128)}, f32[4,1280,160]{1,2,0:T(8,128)}) fusion(f32[4,1280,160]{1,2,0:T(8,128)} %param.6, f32[4,1280,32]{1,2,0:T(8,128)S(1)} %copy-done, f32[4,32,160]{2,1,0:T(8,128)S(1)} %fusion.12, f32[4,1280,160]{1,2,0:T(8,128)} %param.7), kind=kOutput, calls=%fused_computation.7 | convolution fusion | flops 318668800 | bytes 13844480 | tf_op jit(solution)/shard_map/lir,lrw->liw/dot_general | solution.py:35
  (11 shorter events, 0.1 us)
Async XLA Ops:
  7.2 86.3 %all-reduce.3.cloned.1.call-start = ((), (), s32[]{:S(2)}) async-start(), calls=%async_computation | async-start | bytes 1310720 | tf_op jit(solution)/shard_map/psum | solution.py:17
  16.8 240.4 %all-reduce.5.cloned.1.call-start = ((), (), s32[]{:S(2)}) async-start(), calls=%async_computation.1 | async-start | bytes 1310720 | tf_op jit(solution)/shard_map/psum | solution.py:24
  127.5 134.5 %copy-start = (f32[4,1280,32]{1,2,0:T(8,128)S(1)}, f32[4,1280,32]{1,2,0:T(8,128)}, u32[]{:S(2)}) copy-start(f32[4,1280,32]{1,2,0:T(8,128)} %all-reduce.3.cloned.1.call-done) | copy-start | bytes 1966084
Sparse Core Ops, SparseCore 0:
  16.9 76.4 all-reduce.2
  127.6 129.4 all-reduce.4
where the time goes:
time: 276 us
  waiting for transfers between devices  196 us (71%)
  matrix products  28.4 us (10%)
  other arithmetic  25.3 us (9%)
  between operations  14.1 us (5%)
  blocking collectives  10.7 us (4%)
    psum x1, waiting for transfers between devices, on_device(): right = lax.psum(part_right, ('dp', 'tp'))  120 us
    psum x1, waiting for transfers between devices, on_device(): left = lax.psum(part_left, 'dp')  76.5 us
    another operation x4, other arithmetic, on_device(): root = jnp.linalg.cholesky(gram)  11.9 us
    psum x1, blocking collectives, on_device(): gram = lax.psum(part_gram, 'tp')  10.7 us
    another operation x3, other arithmetic, on_device(): lax.linalg.triangular_solve(root, half, left_side=True, lower=True, trans...  9.93 us
    dot_general x1, matrix products, on_device(): jnp.einsum('liw,lwr->lir', own_grads, right_factor.astype(jnp.bfloat16),...  9.56 us
    dot_general x1, matrix products, on_device(): jnp.einsum('liw,lir->lwr', own_grads, small_left, preferred_element_type=...  8.11 us
    dot_general x1, matrix products, on_device(): jnp.einsum('lir,lrw->liw', left, mixed, precision=lax.Precision.HIGHEST)  7.16 us
  transfers between devices with their start and end apart: 2, of which 2 were waited for; matrix products, arithmetic and copies ran while one was open for 4% of the time, Pallas kernels for 0%

commit v1 on v0

v1 whole, which is shorter than its diff:
```python
import functools

import jax
import jax.numpy as jnp
from jax import lax
from jax.experimental import pallas as pl
from jax.experimental.pallas import tpu as pltpu
from jax.sharding import PartitionSpec as P

MESH = pl.DeviceIdType.MESH
HIGH = lax.Precision.HIGHEST
F32 = jnp.float32


def bits_of(n):
    count = n.bit_length() - 1
    assert 1 << count == n
    return count


def swapped_pairs(bits):
    out = list(bits)
    for at in range(0, len(out) - 1, 2):
        out[at], out[at + 1] = out[at + 1], out[at]
    return out


def cut(order, rows, unit=8):
    halved = []
    for bit in order:
        if rows % (2 * unit) == 0:
            halved.append(bit)
            rows //= 2
    return halved, rows


class Reduction:
    def __init__(self, order, dims, shape):
        self.dims = dims
        self.order = [b for b in order if b in dims] + [b for b in order if b not in dims]
        self.shape = shape
        self.full = (2,) * len(dims) + shape
        self.landing = []
        left = len(dims)
        for bit in self.order:
            if bit in dims:
                left -= 1
            self.landing.append((2,) * left + shape)
        self.copies = len(self.order) + len(dims)

    def scratch(self):
        return [pltpu.VMEM(s, F32) for s in [self.full, self.full if self.dims else self.shape] + self.landing]

    def run(self, refs, sems, first, places):
        work, total, landing = refs[0], refs[1], refs[2:]
        send_sem, recv_sem = sems
        slot = first

        def index(fixed, other=None):
            out = []
            for bit in self.dims:
                mine = places[bit][1]
                if bit == other:
                    out.append(1 - mine)
                elif bit in fixed:
                    out.append(mine)
                else:
                    out.append(slice(None))
            return tuple(out) + (slice(None),) * len(self.shape)

        def copy(src, dst, bit, slot):
            return pltpu.make_async_remote_copy(
                src_ref=src, dst_ref=dst, send_sem=send_sem.at[slot], recv_sem=recv_sem.at[slot],
                device_id=places[bit][0], device_id_type=MESH,
            )

        fixed = []
        for step, bit in enumerate(self.order):
            away = index(fixed, bit) if bit in self.dims else index(fixed)
            moving = copy(work.at[away], landing[step], bit, slot)
            slot += 1
            moving.start()
            yield
            moving.wait()
            if bit in self.dims:
                fixed.append(bit)
            own = index(fixed)
            into = total if step == len(self.order) - 1 else work
            into[own] = work[own] + landing[step][...]
        while fixed:
            own = index(fixed)
            bit = fixed.pop()
            moving = copy(total.at[own], total.at[own], bit, slot)
            slot += 1
            moving.start()
            yield
            moving.wait()


def advance(running):
    still = []
    for one in running:
        try:
            next(one)
            still.append(one)
        except StopIteration:
            pass
    return still


def factor_kernel(plan, g_hbm, qt_ref, lit_ref, right_ref, gv, qmask, left_t, right_t, g_sem, send_sem, recv_sem, *bufs):
    layers, rank, width = qt_ref.shape
    lanes = layers * rank
    n_dp, n_tp = plan["n_dp"], plan["n_tp"]
    piece, n_pieces = plan["piece"], plan["n_pieces"]
    me = {"dp": lax.axis_index("dp"), "tp": lax.axis_index("tp")}

    loads = []
    for p in range(n_pieces):
        rows = pl.ds(p * piece, piece)
        load = pltpu.make_async_copy(g_hbm.at[0, :, rows, :], gv.at[:, rows, :], g_sem.at[p])
        load.start()
        loads.append(load)

    places = {}
    for axis, n in (("dp", n_dp), ("tp", n_tp)):
        for b in range(bits_of(n)):
            bit = lax.rem(lax.div(me[axis], 1 << b), 2)
            partner = dict(me)
            partner[axis] = me[axis] + (1 - 2 * bit) * (1 << b)
            places[(axis, b)] = ((partner["dp"], partner["tp"]), bit)
    barrier = pltpu.get_barrier_semaphore()
    for target, _ in places.values():
        pl.semaphore_signal(barrier, inc=1, device_id=target, device_id_type=MESH)

    qt = qt_ref[...].reshape(lanes, width)
    owner = lax.broadcasted_iota(jnp.int32, (lanes, width), 0) // rank
    for l in range(layers):
        qmask[l] = jnp.where(owner == l, qt, 0.0).astype(jnp.bfloat16)
    pl.semaphore_wait(barrier, len(places))

    groups, at = [], 0
    for red in plan["reductions"]:
        count = 2 + len(red.landing)
        groups.append(bufs[at:at + count])
        at += count
    firsts, slot = [], 0
    for red in plan["reductions"]:
        firsts.append(slot)
        slot += red.copies

    def start(i):
        gen = plan["reductions"][i].run(groups[i], (send_sem, recv_sem), firsts[i], places)
        next(gen)
        return gen

    def absorb(p):
        rows = pl.ds(p * piece, piece)
        part = groups[p][1][...].reshape(piece, lanes).T
        left_t[:, rows] = part
        small = part.astype(jnp.bfloat16)
        for l in range(layers):
            out = pl.ds(l * rank, rank)
            term = jnp.dot(small[l * rank:(l + 1) * rank], gv[l, rows, :], preferred_element_type=F32)
            if p == 0:
                right_t[out, :] = term
            else:
                right_t[out, :] = right_t[out, :] + term

    def left_chain(p, gen):
        for _ in gen:
            yield
        absorb(p)

    running = []
    for p in range(n_pieces):
        loads[p].wait()
        rows = pl.ds(p * piece, piece)
        total = None
        for l in range(layers):
            term = lax.dot_general(
                gv[l, rows, :], qmask[l], (((1,), (1,)), ((), ())), preferred_element_type=F32
            )
            total = term if total is None else total + term
        groups[p][0][...] = total.reshape(plan["reductions"][p].full)
        running.append(left_chain(p, start(p)))
        if p >= 2:
            running[:p - 1] = advance(running[:p - 1])
    while running:
        running = advance(running)

    lay = lax.broadcasted_iota(jnp.int32, (layers, rank, lanes), 0)
    row = lax.broadcasted_iota(jnp.int32, (layers, rank, lanes), 1)
    lane = lax.broadcasted_iota(jnp.int32, (layers, rank, lanes), 2)
    block = lane // rank == lay

    def gram_chain():
        whole = left_t[...]
        gram = lax.dot_general(whole, whole, (((1,), (1,)), ((), ())), preferred_element_type=F32, precision=HIGH)
        packed = jnp.sum(jnp.where(block, gram.reshape(layers, rank, lanes), 0.0), axis=0)
        groups[n_pieces][0][...] = packed
        for _ in start_gram():
            yield
        b3 = jnp.where(block, groups[n_pieces][1][...][None], 0.0)
        diag = lane == lay * rank + row
        mean = jnp.sum(jnp.sum(jnp.where(diag, b3, 0.0), axis=1, keepdims=True), axis=2, keepdims=True) / rank
        b3 = jnp.where(diag, b3 + 0.001 * mean, b3)

        def sweep(k, b3):
            lane_k = lane == lay * rank + k
            row_k = row == k
            col = jnp.sum(jnp.where(lane_k, b3, 0.0), axis=2, keepdims=True)
            col = jnp.broadcast_to(col, b3.shape)
            pivot = jnp.sum(jnp.where(row_k, col, 0.0), axis=1, keepdims=True)
            line = jnp.sum(jnp.where(row_k, b3, 0.0), axis=1, keepdims=True)
            inv = 1.0 / pivot
            line = jnp.where(lane_k, inv, line * inv)
            return jnp.where(row_k, line, jnp.where(lane_k, 0.0, b3) - col * line)

        chunks = 4
        for c in range(chunks):
            lo, hi = c * rank // chunks, (c + 1) * rank // chunks
            b3 = lax.fori_loop(lo, hi, sweep, b3)
            yield
        inverse = b3.reshape(lanes, lanes)
        lit_ref[...] = jnp.dot(inverse, left_t[...], preferred_element_type=F32, precision=HIGH) * (1.0 / n_dp)

    def start_gram():
        yield from plan["reductions"][n_pieces].run(
            groups[n_pieces], (send_sem, recv_sem), firsts[n_pieces], places
        )

    gram = gram_chain()
    next(gram)
    running = []
    right = right_t[...].T.reshape((-1, plan["block"], lanes))
    at = 0
    for i, height in enumerate(plan["heights"]):
        k = n_pieces + 1 + i
        groups[k][0][...] = right[:, at:at + height, :].reshape(plan["reductions"][k].full)
        at += height
        running.append(start(k))
    running.append(gram)
    while running:
        running = advance(running)
    parts = []
    for i, height in enumerate(plan["heights"]):
        k = n_pieces + 1 + i
        parts.append(groups[k][1][...].reshape((-1, height, lanes)))
    at = 0
    for part, height in zip(parts, plan["heights"]):
        right_ref[:, at:at + height, :] = part
        at += height


def update_kernel(lit_ref, right_ref, w_ref, m_ref, nw_ref, nb_ref, nm_ref, right_t):
    l = pl.program_id(0)
    own = w_ref.shape[1]
    rank = nb_ref.shape[1]
    width, lanes = right_ref.shape

    @pl.when(l == 0)
    def _():
        right_t[...] = right_ref[...].T

    mine = right_ref[pl.ds(pl.multiple_of(lax.axis_index("dp") * own, 8), own), :]
    lane = lax.broadcasted_iota(jnp.int32, (own, lanes), 1)
    mine = jnp.where(lane // rank == l, mine, 0.0)
    change = jnp.dot(mine, lit_ref[...], preferred_element_type=F32, precision=HIGH)
    momentum = 0.8 * m_ref[0] + change
    nm_ref[0] = momentum
    nw_ref[0] = w_ref[0] - 0.05 * momentum
    basis = right_t[pl.ds(pl.multiple_of(l * rank, 8), rank), :]
    mean = jnp.sum(jnp.sum(basis * basis, axis=1, keepdims=True), axis=0, keepdims=True) / (width * rank)
    nb_ref[0] = basis * lax.rsqrt(mean + 1e-12)


def make_plan(n_dp, n_tp, rows, width, lanes, rank):
    dp = [("dp", b) for b in range(bits_of(n_dp))]
    tp = [("tp", b) for b in range(bits_of(n_tp))]
    piece = 256 if rows % 256 == 0 else rows
    n_pieces = rows // piece
    reductions = []
    for p in range(n_pieces):
        order = dp if p % 2 == 0 else swapped_pairs(dp)
        dims, height = cut(order, piece)
        reductions.append(Reduction(order, sorted(dims, reverse=True), (height, lanes)))
    reductions.append(Reduction(tp, [], (rank, lanes)))
    per = width // n_dp
    dims, block = cut(tp, per)
    tiles = block // 8
    heights = [block] if tiles < 2 else [(tiles + 1) // 2 * 8, tiles // 2 * 8]
    dims = sorted(dp, reverse=True) + sorted(dims, reverse=True)
    for i, height in enumerate(heights):
        order = tp + dp if i % 2 == 0 else swapped_pairs(tp) + swapped_pairs(dp)
        reductions.append(Reduction(order, dims, (height, lanes)))
    return dict(
        n_dp=n_dp, n_tp=n_tp, piece=piece, n_pieces=n_pieces, reductions=reductions, heights=heights, block=block,
        copies=sum(r.copies for r in reductions),
    )


def solution(mesh):
    n_dp, n_tp = mesh.shape["dp"], mesh.shape["tp"]

    def on_device(gradients, right_factor, weights_before, momentum):
        _, layers, rows, width = gradients.shape
        rank = right_factor.shape[2]
        lanes = layers * rank
        own = weights_before.shape[2]
        plan = make_plan(n_dp, n_tp, rows, width, lanes, rank)
        vmem = pl.BlockSpec(memory_space=pltpu.VMEM)
        scratch = [
            pltpu.VMEM((layers, rows, width), jnp.bfloat16),
            pltpu.VMEM((layers, lanes, width), jnp.bfloat16),
            pltpu.VMEM((lanes, rows), F32),
            pltpu.VMEM((lanes, width), F32),
            pltpu.SemaphoreType.DMA((plan["n_pieces"],)),
            pltpu.SemaphoreType.DMA((plan["copies"],)),
            pltpu.SemaphoreType.DMA((plan["copies"],)),
        ]
        for red in plan["reductions"]:
            scratch += red.scratch()
        lit, right = pl.pallas_call(
            functools.partial(factor_kernel, plan),
            out_shape=(
                jax.ShapeDtypeStruct((lanes, rows), F32),
                jax.ShapeDtypeStruct((width // plan["block"], plan["block"], lanes), F32),
            ),
            in_specs=[pl.BlockSpec(memory_space=pl.ANY), vmem],
            out_specs=(vmem, vmem),
            scratch_shapes=scratch,
            compiler_params=pltpu.CompilerParams(
                collective_id=0, has_side_effects=True, vmem_limit_bytes=40 * 1024 * 1024
            ),
            name="factors",
        )(gradients, jnp.swapaxes(right_factor, 1, 2))
        right = right.reshape(width, lanes)
        one = lambda a, b: pl.BlockSpec((1, a, b), lambda l: (l, 0, 0))
        whole = lambda a, b: pl.BlockSpec((a, b), lambda l: (0, 0))
        new_w, new_b, new_m = pl.pallas_call(
            update_kernel,
            grid=(layers,),
            out_shape=(
                jax.ShapeDtypeStruct((layers, own, rows), F32),
                jax.ShapeDtypeStruct((layers, rank, width), F32),
                jax.ShapeDtypeStruct((layers, own, rows), F32),
            ),
            in_specs=[whole(lanes, rows), whole(width, lanes), one(own, rows), one(own, rows)],
            out_specs=(one(own, rows), one(rank, width), one(own, rows)),
            scratch_shapes=[pltpu.VMEM((lanes, width), F32)],
            compiler_params=pltpu.CompilerParams(dimension_semantics=("arbitrary",)),
            name="update",
        )(lit, right, jnp.swapaxes(weights_before, 1, 2), jnp.swapaxes(momentum, 1, 2))
        return tuple(jnp.swapaxes(a, 1, 2) for a in (new_w, new_b, new_m))

    return jax.shard_map(
        on_device,
        mesh=mesh,
        in_specs=(P("dp", None, "tp", None), P(), P(None, "tp", "dp"), P(None, "tp", "dp")),
        out_specs=(P(None, "tp", "dp"), P(), P(None, "tp", "dp")),
        check_vma=False,
    )
```

time: 276 us -> 86.6 us (0.31)
  waiting for transfers between devices: 196 us -> 0 us
  Pallas kernels: 0 us -> 82.9 us
  matrix products: 28.4 us -> 0 us
  other arithmetic: 25.3 us -> 0 us
  between operations: 14.1 us -> 0.66 us
  blocking collectives: 10.7 us -> 0 us
    psum x2 -> x0, waiting for transfers between devices: 196 us -> none  [the longest x1 120 us: on_device(): right = lax.psum(part_right, ('dp', 'tp'))]
    pallas_call x0 -> x2, Pallas kernels: none -> 82.9 us  [the longest x1 74.6 us: on_device(): pl.pallas_call(functools.partial(factor_kernel, plan), out_shape=(jax.Sha...]
    dot_general x4 -> x0, matrix products: 26.8 us -> none  [the longest x1 9.56 us: on_device(): jnp.einsum('liw,lwr->lir', own_grads, right_factor.astype(jnp.bfloat16),...]
    another operation x7 -> x0, other arithmetic: 21.8 us -> none  [the longest x4 11.9 us: on_device(): root = jnp.linalg.cholesky(gram)]
    psum x1 -> x0, blocking collectives: 10.7 us -> none  [on_device(): gram = lax.psum(part_gram, 'tp')]
  transfers between devices with their start and end apart: 2 -> 0, of which waited for: 2 -> 0; matrix products, arithmetic and copies ran while one was open for 4% -> 0% of each run, Pallas kernels for 0% -> 0%
where the time goes in v1:
time: 86.6 us; the launch traced here: 86.4 us
  Pallas kernels  82.9 us (96%)
  local copies, waits for them, and re-layouts  2.75 us (3%)
    pallas_call x1, Pallas kernels, on_device(): pl.pallas_call(functools.partial(factor_kernel, plan), out_shape=(jax.Sha...  74.6 us
    pallas_call x1, Pallas kernels, on_device(): pl.pallas_call(update_kernel, grid=(layers,), out_shape=(jax.ShapeDtypeSt...  8.32 us
    unnamed x6, local copies, waits for them, and re-layouts  2.75 us

profile of v1, /device:TPU:0, one launch (start us, length us, event | category | flops | bytes accessed | tf_op | source)
XLA Modules:
  0.0 86.4 jit_solution(14587125702455212235)
XLA Ops:
  0.6 0.0 copy-start
  0.6 1.1 %copy-done = f32[4,1280,32]{1,2,0:T(8,128)S(1)} copy-done((f32[4,1280,32]{1,2,0:T(8,128)S(1)}, f32[4,1280,32]{1,2,0:T(8,128)}, u32[]{:S(2)}) %copy-start) | copy-done | bytes 655384
  1.7 74.6 %factors.1 = (f32[128,1280]{1,0:T(8,128)S(1)}, f32[32,40,128]{2,1,0:T(8,128)S(1)}) custom-call(bf16[1,4,1280,1280]{3,2,1,0:T(8,128)(2,1)} %g_hbm.1, f32[4,32,1280]{2,1,0:T(8,128)S(1)} %bitcast.7), custom_call_target="tpu_custom_call" | custom-call | tf_op jit(solution)/shard_map/factors/pallas_call | solution.py:324
  76.4 0.0 copy-start.1
  76.4 0.8 copy-done.1
  77.2 0.0 copy-start.2
  77.2 0.8 copy-done.2
  78.0 8.3 %update.1 = (f32[4,160,1280]{2,1,0:T(8,128)}, f32[4,32,1280]{2,1,0:T(8,128)}, f32[4,160,1280]{2,1,0:T(8,128)}) custom-call(f32[128,1280]{1,0:T(8,128)} %copy-done.1, f32[1280,128]{1,0:T(8,128)} %bitcast.8, f32[4,160,1280]{2,1,0:T(8,128)} %bitcast.9, f32[4,160,1280]{2,1,0:T(8,128)} %bitcast.10), custom_call_target="tpu_custom_call" | custom-call | tf_op jit(solution)/shard_map/update/pallas_call | solution.py:341
Async XLA Ops:
  0.6 1.1 %copy-start = (f32[4,1280,32]{1,2,0:T(8,128)S(1)}, f32[4,1280,32]{1,2,0:T(8,128)}, u32[]{:S(2)}) copy-start(f32[4,1280,32]{1,2,0:T(8,128)} %param.5) | copy-start | bytes 1966084
  76.4 0.8 copy-start.1
  77.2 0.8 copy-start.2

commit v2 on v1

--- a/solution.py
+++ b/solution.py
@@ -133,10 +133,10 @@
     for target, _ in places.values():
         pl.semaphore_signal(barrier, inc=1, device_id=target, device_id_type=MESH)
 
-    qt = qt_ref[...].reshape(lanes, width)
-    owner = lax.broadcasted_iota(jnp.int32, (lanes, width), 0) // rank
+    q = qt_ref[...].reshape(lanes, width).T
+    owner = lax.broadcasted_iota(jnp.int32, (width, lanes), 1) // rank
     for l in range(layers):
-        qmask[l] = jnp.where(owner == l, qt, 0.0).astype(jnp.bfloat16)
+        qmask[l] = jnp.where(owner == l, q, 0.0).astype(jnp.bfloat16)
     pl.semaphore_wait(barrier, len(places))
 
     groups, at = [], 0
@@ -178,9 +178,7 @@
         rows = pl.ds(p * piece, piece)
         total = None
         for l in range(layers):
-            term = lax.dot_general(
-                gv[l, rows, :], qmask[l], (((1,), (1,)), ((), ())), preferred_element_type=F32
-            )
+            term = jnp.dot(gv[l, rows, :], qmask[l], preferred_element_type=F32)
             total = term if total is None else total + term
         groups[p][0][...] = total.reshape(plan["reductions"][p].full)
         running.append(left_chain(p, start(p)))
@@ -230,8 +228,6 @@
             groups[n_pieces], (send_sem, recv_sem), firsts[n_pieces], places
         )
 
-    gram = gram_chain()
-    next(gram)
     running = []
     right = right_t[...].T.reshape((-1, plan["block"], lanes))
     at = 0
@@ -240,7 +236,7 @@
         groups[k][0][...] = right[:, at:at + height, :].reshape(plan["reductions"][k].full)
         at += height
         running.append(start(k))
-    running.append(gram)
+    running += advance([gram_chain()])
     while running:
         running = advance(running)
     parts = []
@@ -278,7 +274,7 @@
 def make_plan(n_dp, n_tp, rows, width, lanes, rank):
     dp = [("dp", b) for b in range(bits_of(n_dp))]
     tp = [("tp", b) for b in range(bits_of(n_tp))]
-    piece = 256 if rows % 256 == 0 else rows
+    piece = rows // 2 if rows % 256 == 0 else rows
     n_pieces = rows // piece
     reductions = []
     for p in range(n_pieces):
@@ -312,7 +308,7 @@
         vmem = pl.BlockSpec(memory_space=pltpu.VMEM)
         scratch = [
             pltpu.VMEM((layers, rows, width), jnp.bfloat16),
-            pltpu.VMEM((layers, lanes, width), jnp.bfloat16),
+            pltpu.VMEM((layers, width, lanes), jnp.bfloat16),
             pltpu.VMEM((lanes, rows), F32),
             pltpu.VMEM((lanes, width), F32),
             pltpu.SemaphoreType.DMA((plan["n_pieces"],)),
@@ -349,7 +345,9 @@
             in_specs=[whole(lanes, rows), whole(width, lanes), one(own, rows), one(own, rows)],
             out_specs=(one(own, rows), one(rank, width), one(own, rows)),
             scratch_shapes=[pltpu.VMEM((lanes, width), F32)],
-            compiler_params=pltpu.CompilerParams(dimension_semantics=("arbitrary",)),
+            compiler_params=pltpu.CompilerParams(
+                dimension_semantics=("arbitrary",), vmem_limit_bytes=20 * 1024 * 1024
+            ),
             name="update",
         )(lit, right, jnp.swapaxes(weights_before, 1, 2), jnp.swapaxes(momentum, 1, 2))
         return tuple(jnp.swapaxes(a, 1, 2) for a in (new_w, new_b, new_m))

time: 86.6 us -> 78.2 us (0.903)
  Pallas kernels: 82.9 us -> 76.3 us
  local copies, waits for them, and re-layouts: 2.75 us -> 1.09 us
    pallas_call x1, Pallas kernels: 74.6 us -> 71.2 us  [on_device(): pl.pallas_call(functools.partial(factor_kernel, plan), out_shape=(jax.Sha...]
    pallas_call x1, Pallas kernels: 8.32 us -> 5.09 us  [on_device(): pl.pallas_call(update_kernel, grid=(layers,), out_shape=(jax.ShapeDtypeSt...]
    unnamed x6, local copies, waits for them, and re-layouts: 2.75 us -> 1.09 us
where the time goes in v2:
time: 78.2 us; the launch traced here: 78 us
  Pallas kernels  76.3 us (98%)
  local copies, waits for them, and re-layouts  1.09 us (1%)
    pallas_call x1, Pallas kernels, on_device(): pl.pallas_call(functools.partial(factor_kernel, plan), out_shape=(jax.Sha...  71.2 us
    pallas_call x1, Pallas kernels, on_device(): pl.pallas_call(update_kernel, grid=(layers,), out_shape=(jax.ShapeDtypeSt...  5.09 us

profile of v2, /device:TPU:0, one launch (start us, length us, event | category | flops | bytes accessed | tf_op | source)
XLA Modules:
  0.0 78.0 jit_solution(11961041710753315898)
XLA Ops:
  0.6 0.0 copy-start.2
  0.6 1.1 %copy-done.2 = f32[4,1280,32]{1,2,0:T(8,128)S(1)} copy-done((f32[4,1280,32]{1,2,0:T(8,128)S(1)}, f32[4,1280,32]{1,2,0:T(8,128)}, u32[]{:S(2)}) %copy-start.2) | copy-done | bytes 655384
  1.7 0.0 copy-start
  1.7 0.0 copy-start.1
  1.7 71.2 %factors.1 = (f32[128,1280]{1,0:T(8,128)S(1)}, f32[32,40,128]{2,1,0:T(8,128)S(1)}) custom-call(bf16[1,4,1280,1280]{3,2,1,0:T(8,128)(2,1)} %g_hbm.1, f32[4,32,1280]{2,1,0:T(8,128)S(1)} %bitcast.9), custom_call_target="tpu_custom_call" | custom-call | tf_op jit(solution)/shard_map/factors/pallas_call | solution.py:320
  72.9 0.0 copy-done
  72.9 0.0 copy-done.1
  72.9 5.1 %update.1 = (f32[4,160,1280]{2,1,0:T(8,128)}, f32[4,32,1280]{2,1,0:T(8,128)}, f32[4,160,1280]{2,1,0:T(8,128)}) custom-call(f32[128,1280]{1,0:T(8,128)S(1)} %get-tuple-element.8.lit_ref, f32[1280,128]{1,0:T(8,128)S(1)} %bitcast.10, f32[4,160,1280]{2,1,0:T(8,128)S(1)} %bitcast.7, f32[4,160,1280]{2,1,0:T(8,128)S(1)} %bitcast.8), custom_call_target="tpu_custom_call" | custom-call | tf_op jit(solution)/shard_map/update/pallas_call | solution.py:337
Async XLA Ops:
  0.6 1.1 %copy-start.2 = (f32[4,1280,32]{1,2,0:T(8,128)S(1)}, f32[4,1280,32]{1,2,0:T(8,128)}, u32[]{:S(2)}) copy-start(f32[4,1280,32]{1,2,0:T(8,128)} %param.5) | copy-start | bytes 1966084
  1.7 71.2 %copy-start = (f32[4,1280,160]{1,2,0:T(8,128)S(1)}, f32[4,1280,160]{1,2,0:T(8,128)}, u32[]{:S(2)}) copy-start(f32[4,1280,160]{1,2,0:T(8,128)} %param.6) | copy-start | bytes 9830404
  1.7 71.2 %copy-start.1 = (f32[4,1280,160]{1,2,0:T(8,128)S(1)}, f32[4,1280,160]{1,2,0:T(8,128)}, u32[]{:S(2)}) copy-start(f32[4,1280,160]{1,2,0:T(8,128)} %param.7) | copy-start | bytes 9830404
